TPU v7x, 128 devices: a whole 4x4x4 slice. The times are simulated.
128 devices in a mesh: batch: 1, cols: 2 (over core), rows: 64 (over z, y, x).
Axes of the slice: x: 4, y: 4, z: 4, core: 2. Of those that a mesh axis runs over, the one named last changes fastest.
Arguments:
- frames: bfloat16 [16, 2, 2048, 64, 64], P(None, 'batch', 'rows', 'cols')
- w_x: bfloat16 [3, 3, 64, 256], replicated
- w_h: bfloat16 [3, 3, 64, 256], replicated
- gate_bias: float32 [256], replicated
- h_init: bfloat16 [2, 2048, 64, 64], P('batch', 'rows', 'cols')
- c_init: float32 [2, 2048, 64, 64], P('batch', 'rows', 'cols')
Outputs:
- output 1: bfloat16 [16, 2, 2048, 64, 64], P(None, 'batch', 'rows', 'cols')
- output 2: float32 [2, 2048, 64, 64], P('batch', 'rows', 'cols')
All inputs are finite; a program needn't handle non-finite values.
Results may differ from a plain program's by a relative error of at most 0.00242049.
Values are sent between devices in bfloat16 or wider.
A program may use at most 1 GiB of HBM per device.

v0:
```python
import functools

import jax
import jax.numpy as jnp
from jax import lax
from jax.experimental import pallas as pl
from jax.experimental.pallas import tpu as pltpu
from jax.sharding import PartitionSpec as P

MESH = pl.DeviceIdType.MESH
CH = 64
LANES = 128
COLS = 8
PIECE = 4
RING = 8
BLOCKS = (7, 9)
LATE = (2, 3)
BORDER = 3
FAR = 16


def cuts(lo, hi, size=PIECE):
    n = max(1, (hi - lo) // size)
    edges = [lo + i * size for i in range(n)] + [hi]
    return list(zip(edges[:-1], edges[1:]))


def even_cuts(lo, hi):
    n = max(1, round((hi - lo) / BORDER))
    edges = [lo + (hi - lo) * i // n for i in range(n + 1)]
    return list(zip(edges[:-1], edges[1:]))


class Plan:
    def __init__(self, blocks, T, R, W):
        assert sum(blocks) == T
        self.blocks, self.T, self.R, self.W, self.HW, self.HG = blocks, T, R, W, W // 2, W // 2 // COLS
        self.K = max(blocks)
        self.first = [sum(blocks[:b]) for b in range(len(blocks))]
        self.of = [(b, o) for b, k in enumerate(blocks) for o in range(k)]
        self.xrows = [blocks[b] - o for b, o in self.of]
        self.xat = [sum(self.xrows[:t]) for t in range(T + 1)]
        self.parts = [[(0, 1), (1, 2), (2, 3), (3, k)] if b == 0 else [(0, k)] for b, k in enumerate(blocks)]
        self.hat = [sum(blocks[:b]) for b in range(len(blocks) + 1)]
        self.cat = [sum(k - 1 for k in blocks[:b]) for b in range(len(blocks) + 1)]
        ends = [0, 1, 3, blocks[0] + 1, T]
        self.groups = [(a, e) for a, e in zip(ends[:-1], ends[1:]) if e > a]


def kernel(plan, n_rows, frames, w_x, w_h, bias_in, h_init, c_init, hout, hpeer, cout, cpeer,
           bias, hgo, cgo, cgp, cin, xgo, xin, hst, cst, xh_even, xh_odd, cbuf, shift, wbuf,
           xs_ref, xr_ref, hs_ref, hr_ref, cs_ref, cr_ref,
           s_w, s_i, s_ir, s_is, s_x, s_xr, s_xs, s_b, s_bs, s_or, s_os, here_sem):
    T, R, W, HW, HG = plan.T, plan.R, plan.W, plan.HW, plan.HG
    PAD = plan.K
    NB = len(plan.blocks)
    s = lax.axis_index("cols")
    n = lax.axis_index("rows")
    p = 1 - s
    mine, theirs = pl.ds(s * HG, HG), pl.ds(p * HG, HG)
    mine_c, theirs_c = [pl.ds(pl.multiple_of(i * HW, HW), HW) for i in (s, p)]
    has_up, has_dn = n > 0, n < n_rows - 1
    bf, f32 = jnp.bfloat16, jnp.float32

    def local(src, dst, sem):
        return pltpu.make_async_copy(src, dst, sem)

    def remote(src, dst, ssem, rsem, dev):
        return pltpu.make_async_remote_copy(
            src_ref=src, dst_ref=dst, send_sem=ssem, recv_sem=rsem, device_id=dev, device_id_type=MESH)

    peer = {"cols": p}
    side_dev = [{"rows": n - 1}, {"rows": n + 1}]
    side_ok = [has_up, has_dn]

    def each_side(do):
        for side in range(2):
            @pl.when(side_ok[side])
            def _():
                do(side)

    barrier = pltpu.get_barrier_semaphore()

    def signal(dev):
        pl.semaphore_signal(barrier, inc=1, device_id=dev, device_id_type=MESH)

    signal(peer)

    @pl.when(has_up)
    def _():
        signal(side_dev[0])


    h_own = local(h_init.at[s], hst.at[:, mine], s_i.at[0])
    c_own = local(c_init.at[s], cst, s_i.at[1])
    x_own = [local(frames.at[a:e, s], xin.at[a:e, :, mine], s_x.at[g]) for g, (a, e) in enumerate(plan.groups)]
    h_got = local(h_init.at[p], hgo, s_i.at[2])
    c_got = local(c_init.at[p], cgo, s_i.at[3])
    x_got = [local(frames.at[a:e, p], xgo.at[a:e], s_i.at[4 + g]) for g, (a, e) in enumerate(plan.groups[:2])]
    w_copies = [local(w_h, wbuf.at[0:9, 0], s_w.at[0]), local(w_x, wbuf.at[0:9, 1], s_w.at[1]),
                local(bias_in, bias, s_w.at[2])]
    for c in [h_got, x_got[0], c_got, h_own, x_own[0], c_own, *w_copies, x_got[1], *x_own[1:]]:
        c.start()
    pl.semaphore_wait(barrier, 1 + has_dn.astype(jnp.int32))

    @pl.when(has_dn)
    def _():
        pl.semaphore_signal(here_sem, inc=1, device_id=side_dev[1], device_id_type=MESH)


    h_push = remote(hgo, hst.at[:, mine], s_is.at[0], s_ir.at[0], peer)
    c_push = remote(cgp, cin, s_is.at[1], s_ir.at[1], peer)
    x_push = [remote((xgo if g < 2 else frames.at[:, p]).at[a:e], xin.at[a:e, :, mine], s_xs.at[g], s_xr.at[g], peer)
              for g, (a, e) in enumerate(plan.groups)]
    for got, push in [(h_got, h_push), (x_got[0], x_push[0]), (c_got, c_push), (x_got[1], x_push[1])]:
        got.wait()
        if push is c_push:
            cgp[...] = jnp.concatenate([cgo[:, :HW // 2], cgo[:, HW // 2:]], axis=2)
        push.start()
    for push in x_push[2:]:
        push.start()

    shift[...] = jnp.zeros_like(shift)
    low = lax.broadcasted_iota(jnp.int32, (1, LANES), 1) < CH
    low_half = low_row = low
    turn = [0]
    scale = jnp.where(low_row, 0.5, 1.0)
    lift = jnp.where(low_row, 0.5, 0.0)

    for c in w_copies:
        c.wait()
    for tap in range(9):
        for half in range(2):
            tile = wbuf[tap, half, :, 0:LANES]
            wbuf[tap, half, :, 0:LANES] = jnp.concatenate([tile[:, CH:], tile[:, :CH]], axis=1)
    b_all = bias[...]
    rest = jnp.concatenate([b_all[:, CH:LANES], b_all[:, :CH], b_all[:, LANES:]], axis=1)
    row = lax.broadcasted_iota(jnp.int32, (CH, 4 * CH), 0)
    rows = jnp.zeros((CH, 4 * CH), f32)
    for i in range(3):
        top = (rest * (1 - 2.0 ** -8)).astype(bf).astype(f32) if i == 0 else rest.astype(bf).astype(f32)
        rows = jnp.where(row == i, top, rows)
        rest = rest - top
    wbuf[9, 0] = rows.astype(bf)
    wbuf[9, 1] = jnp.zeros((CH, 4 * CH), bf)
    ones = jnp.where(lax.broadcasted_iota(jnp.int32, (1, LANES), 1) < 3, 1.0, 0.0).astype(bf)

    def pack(v):
        return jnp.concatenate([v[:, :HG], v[:, HG:]], axis=3)

    def unpack(v):
        return jnp.concatenate([v[..., :CH], v[..., CH:]], axis=1)

    def masked(r, v):
        if 0 <= r < R:
            return v
        return lax.select(jnp.broadcast_to(has_up if r < 0 else has_dn, v.shape), v, jnp.zeros_like(v))

    def emit(t, lo, hi, hx):
        nxt = xh_even if t % 2 == 0 else xh_odd
        at, to = slot(lo, hi), cells_of(lo, hi)
        shift[at, 8:8 + W, :] = hx.reshape(hi - lo, W, LANES)
        nxt[1, to] = hx.astype(bf)
        nxt[0, to] = shift[at, 7:7 + W, :].reshape(hx.shape).astype(bf)
        nxt[2, to] = shift[at, 9:9 + W, :].reshape(hx.shape).astype(bf)

    def cells_of(lo, hi):
        return slice((lo + PAD) * W, (hi + PAD) * W)

    def slot(lo, hi):
        if turn[0] + hi - lo > RING:
            turn[0] = 0
        turn[0] += hi - lo
        return slice(turn[0] - (hi - lo), turn[0])

    def flat(v):
        return v.reshape(-1, v.shape[-1])

    def x_rows(t, lo, hi):
        if lo >= 0 and hi <= R:
            return flat(xin[t, lo:hi].astype(f32))
        side, i = (0, lo + plan.xrows[t]) if lo < 0 else (1, lo - R)
        return flat(unpack(xr_ref[side, plan.xat[t] + i:plan.xat[t] + i + hi - lo].astype(f32)))

    def wait_x(g):
        if g < len(plan.groups):
            x_own[g].wait()
            x_push[g].wait_recv()

    def border(b, kind, side):
        f = plan.first[b]
        if kind < 2:
            src, dst, at = [(hs_ref, hr_ref, plan.hat), (cs_ref, cr_ref, plan.cat)][kind]
            at, end = at[b], at[b + 1]
        else:
            src, dst = xs_ref, xr_ref
            at, end = [plan.xat[f + o] for o in plan.parts[b][kind - 2]]
        return remote(src.at[side, at:end], dst.at[1 - side, at:end],
                      s_bs.at[min(kind, 2), side], s_b.at[kind, 1 - side, b], side_dev[side])

    def pack_x(t0, t1):
        for side in range(2):
            for t in range(t0, t1):
                m = plan.xrows[t]
                lo = 0 if side == 0 else R - m
                xs_ref[side, plan.xat[t]:plan.xat[t] + m] = pack(xin[t, lo:lo + m])

    def start_border(b, *kinds):
        each_side(lambda side: [border(b, kind, side).start() for kind in kinds])

    far = lax.rem(n, FAR) == 0

    def start_first(side, late, *kinds):
        ok = has_dn if side else jnp.logical_and(has_up, far if late else jnp.logical_not(far))

        @pl.when(ok)
        def _():
            if not side and 0 in kinds:
                pl.semaphore_wait(here_sem, 1)
            for kind in kinds:
                border(0, kind, side).start()

    def wait_border(b, *kinds):
        each_side(lambda side: [border(b, kind, 1 - side).wait_recv() for kind in kinds])

    def pack_h(b, h_rows):
        k = plan.blocks[b]
        for side in range(2):
            lo = 0 if side == 0 else R - k
            hs_ref[side, plan.hat[b]:plan.hat[b] + k] = pack(h_rows[lo:lo + k])

    def pack_c(b):
        k = plan.blocks[b]
        for side in range(2):
            lo = PAD if side == 0 else PAD + R - (k - 1)
            c = cbuf[lo:lo + k - 1]
            cs_ref[side, plan.cat[b]:plan.cat[b] + k - 1] = jnp.where(low_half, c[:, :HW], c[:, HW:])

    weights = wbuf[...].reshape(10 * LANES, 4 * CH)

    def dot(t, lo, hi):
        cur = xh_even if t % 2 == 0 else xh_odd
        taps = [cur[dc, cells_of(lo + dr - 1, hi + dr - 1)] for dr in range(3) for dc in range(3)]
        taps.append(jnp.broadcast_to(ones, taps[0].shape))
        return jnp.dot(jnp.concatenate(taps, axis=1), weights, preferred_element_type=f32)

    def cells(t, lo, hi, gates):
        fi = jnp.tanh(gates[:, :LANES] * 0.5) * 0.5 + 0.5
        og = jnp.tanh(gates[:, LANES:] * scale) * scale + lift
        at = slice(lo + PAD, hi + PAD)
        prod = fi * lax.select(jnp.broadcast_to(low, og.shape), cbuf[at].reshape(og.shape), og)
        c = prod + pltpu.roll(prod, CH, 1)
        h = (og * jnp.tanh(c))[:, :CH]
        if t == T - 1:
            c = c.reshape(hi - lo, 2, 2, HW // 2, LANES)
            for half in range(2):
                both = c[:, half, 0]
                cout[half, lo:hi] = lax.select(jnp.broadcast_to(low, both.shape), both, c[:, half, 1])
        else:
            cbuf[at] = c.reshape(hi - lo, W, LANES)
        for a, e in ((lo, min(hi, 0)), (max(lo, 0), min(hi, R)), (max(lo, R), hi)):
            if a >= e:
                continue
            part = h[(a - lo) * W:(e - lo) * W]
            if a >= 0 and e <= R:
                hout[t, a:e] = part.reshape(e - a, 2 * HG, COLS, CH).astype(bf)
            if t < T - 1:
                emit(t + 1, a, e, masked(a, jnp.concatenate([part, x_rows(t + 1, a, e)], axis=1)))

    pending = []

    def piece(at, ahead=1):
        t, lo, hi = at
        while any(u == t - 1 and a <= hi and lo <= e for u, a, e, _ in pending):
            cells(*pending.pop(0))
        pending.append((*at, dot(*at)))
        flush(ahead)

    def flush(left=0):
        while len(pending) > left:
            cells(*pending.pop(0))

    def push_h(t0, t1, lo=0, hi=R):
        rows = slice(lo, hi)
        remote(hout.at[t0:t1, rows, theirs], hpeer.at[t0:t1, rows], s_os.at[0], s_or.at[0], peer).start()

    def push_c(lo, hi):
        remote(cout.at[p, lo:hi], cpeer.at[lo:hi], s_os.at[1], s_or.at[1], peer).start()

    for c in [h_own, x_own[0]]:
        c.wait()
    for c in [h_push, x_push[0]]:
        c.wait_recv()
    pack_h(0, hst)
    pack_x(0, 1)
    start_first(1, 0, 0, 2)
    start_first(0, 0, 0, 2)
    for lo, hi in cuts(0, R):
        emit(0, lo, hi, jnp.concatenate([flat(hst[lo:hi].astype(f32)), x_rows(0, lo, hi)], axis=1))

    for b, k in enumerate(plan.blocks):
        f = plan.first[b]
        last = b + 1 == NB

        def inner(o):
            if o == 0:
                got = [*cuts(k + 1, R - 1 - k), *cuts(1, k + 1), *cuts(R - 1 - k, R - 1)]
            else:
                got = cuts(o + 1, R - 1 - o)
                got = got[1:-1] + [got[0], got[-1]]
            return [(f + o, lo, hi) for lo, hi in got]

        early = [at for o in range(k) for at in inner(o)]
        late = early[len(early) - LATE[b]:]
        for o in range(k):
            pieces = [at for at in early[:len(early) - LATE[b]] if at[0] == f + o]
            first = 0
            if o == 0 and b:
                piece(pieces[0], 9)
                flush(1)
                pack_h(b, hout.at[f - 1])
                pack_c(b)
                start_border(b, 0, 1)
                first = 1
            if b == 0 and o == 0:
                for at in pieces[:2]:
                    piece(at, 9)
                c_own.wait()
                c_push.wait_recv()
                wait_x(1)
                for at in pieces[2:4]:
                    piece(at, 9)
                c0, got = cst[...], cin[...]
                cbuf[PAD:PAD + R, mine_c] = jnp.concatenate([c0, c0], axis=2)
                swapped, keep = pltpu.roll(got, CH, 2), jnp.broadcast_to(low, got.shape)
                both = [lax.select(keep, got, swapped), lax.select(keep, swapped, got)]
                cbuf[PAD:PAD + R, theirs_c] = jnp.concatenate(both, axis=1)
                pack_c(0)
                pack_x(1, 3)
                start_first(1, 0, 1, 3, 4)
                start_first(0, 0, 1, 3, 4)
                first = 4
            if b == 0 and o == 2:
                for at in pieces[:2]:
                    piece(at, 9)
                flush(2)
                wait_x(2)
                for at in pieces[2:4]:
                    piece(at, 9)
                pack_x(3, k)
                for side in range(2):
                    start_first(side, 0, 5)
                start_first(0, 1, 5)
                first = 4
            if b == 0 and o == 4:
                for at in pieces[:2]:
                    piece(at, 9)
                flush(2)
                wait_x(3)
                todo = plan.blocks[1]
                share = -(-todo // len(pieces[2:]))
                for i, at in enumerate(pieces[2:]):
                    piece(at)
                    pack_x(k + min(i * share, todo), k + min((i + 1) * share, todo))
                start_border(1, 2)
                first = len(pieces)
            for at in pieces[first:]:
                piece(at)
            if b == 0 and o == 0:
                start_first(0, 1, 0, 2, 1, 3, 4)
            if o == 0 and b and not last:
                pack_x(f + k, f + k + plan.blocks[b + 1])
        wait_border(b, 0, 2)
        if b and not last:
            start_border(b + 1, 2)
        if b:
            push_h(plan.first[b - 1], f)
        piece(late.pop(0), 3)
        for side in range(2):
            lo = -k if side == 0 else R
            h = flat(unpack(hr_ref[side, plan.hat[b]:plan.hat[b] + k].astype(f32)))
            for a, e in cuts(lo, lo + k):
                part = h[(a - lo) * W:(e - lo) * W]
                emit(f, a, e, masked(a, jnp.concatenate([part, x_rows(f, a, e)], axis=1)))
        for o in range(k):
            m = k - 1 - o
            top, bottom = even_cuts(-m, o + 1), even_cuts(R - 1 - o, R + m)
            for lo, hi in top:
                piece((f + o, lo, hi), 9 if o == 0 else 1)
                if lo != top[0][0]:
                    continue
                if b == 0 and o in (1, 2):
                    wait_border(0, 3 + o)
                if last and o == k // 2:
                    push_h(f, f + o)
                if last and o == k - 2:
                    push_h(f + k // 2, f + o)
                    push_h(T - 1, T, k, R - k)
                    push_c(k, R - k)
                if last and o == k - 1:
                    push_h(T - 2, T - 1)
            for lo, hi in bottom:
                piece((f + o, lo, hi), 9 if o == 0 else 1)
            if o == 0:
                wait_border(b, 1, *(() if b else (3,)))
                for side in range(2):
                    lo = PAD - (k - 1) if side == 0 else PAD + R
                    packed = cr_ref[side, plan.cat[b]:plan.cat[b] + k - 1]
                    both = jnp.concatenate([packed, pltpu.roll(packed, CH, 2)], axis=1)
                    cbuf[lo:lo + k - 1] = both
                while late:
                    piece(late.pop(0), 3)
        assert not late
    flush()
    k = plan.blocks[-1]
    for lo, hi in ((0, k), (R - k, R)):
        push_h(T - 1, T, lo, hi)
        push_c(lo, hi)

    for c in [h_push, c_push, *x_push]:
        c.wait_send()

    def wait_sends(side):
        for kind, ref in enumerate((hs_ref, cs_ref, xs_ref)):
            local(ref.at[side], ref.at[side], s_bs.at[kind, side]).wait()

    each_side(wait_sends)
    for sem in (s_os, s_or):
        local(hpeer, hpeer, sem.at[0]).wait()
        local(cpeer, cpeer, sem.at[1]).wait()


def store(hout, hpeer, cout, cpeer, h_all, c_final, c_tile, sems):
    s = lax.axis_index("cols")
    HG = hpeer.shape[2]
    copies = [pltpu.make_async_copy(hout.at[:, :, pl.ds(s * HG, HG)], h_all.at[:, s], sems.at[0]),
              pltpu.make_async_copy(hpeer, h_all.at[:, 1 - s], sems.at[1]),
              pltpu.make_async_copy(c_tile.at[0], c_final.at[s], sems.at[2]),
              pltpu.make_async_copy(c_tile.at[1], c_final.at[1 - s], sems.at[3])]
    for c in copies[:2]:
        c.start()
    for i, packed in enumerate((cout[s], cpeer[...])):
        c_tile[i] = jnp.concatenate([packed[:, :, :CH], packed[:, :, CH:]], axis=1)
    for c in copies[2:]:
        c.start()
    for c in copies:
        c.wait()


def run(blocks, n_rows, frames, w_x, w_h, gate_bias, h_init, c_init):
    T, S, R, HW = frames.shape[:4]
    W, HG = 2 * HW, HW // COLS
    plan = Plan(blocks, T, R, W)
    NB, PAD, G = len(blocks), plan.K, len(plan.groups)
    bf, f32 = jnp.bfloat16, jnp.float32
    vm, dma = pltpu.VMEM, pltpu.SemaphoreType.DMA
    hbm = pl.BlockSpec(memory_space=pltpu.HBM)
    vmem = pl.BlockSpec(memory_space=pltpu.VMEM)
    tiled = frames.reshape(T, S, R, HG, COLS, CH)
    parts = pl.pallas_call(
        functools.partial(kernel, plan, n_rows),
        out_shape=(vm((T, R, 2 * HG, COLS, CH), bf), vm((T, R, HG, COLS, CH), bf),
                   vm((2, R, HW // 2, LANES), f32), vm((R, HW // 2, LANES), f32)),
        in_specs=[hbm] * 6,
        out_specs=(vmem,) * 4,
        scratch_shapes=[
            vm((1, 4 * CH), f32), vm((R, HG, COLS, CH), bf), vm((R, HW, CH), f32),
            vm((R, HW // 2, LANES), f32), vm((R, HW // 2, LANES), f32),
            vm((plan.groups[1][1], R, HG, COLS, CH), bf),
            vm((T, R, 2 * HG, COLS, CH), bf), vm((R, 2 * HG, COLS, CH), bf), vm((R, HW, CH), f32),
            vm((3, (R + 2 * PAD) * W, LANES), bf), vm((3, (R + 2 * PAD) * W, LANES), bf),
            vm((R + 2 * PAD, W, LANES), f32), vm((RING, W + 16, LANES), f32), vm((10, 2, CH, 4 * CH), bf),
            vm((2, plan.xat[-1], HG, COLS, LANES), bf), vm((2, plan.xat[-1], HG, COLS, LANES), bf),
            vm((2, plan.hat[-1], HG, COLS, LANES), bf), vm((2, plan.hat[-1], HG, COLS, LANES), bf),
            vm((2, plan.cat[-1], HW, LANES), f32), vm((2, plan.cat[-1], HW, LANES), f32),
            dma((3,)), dma((6,)), dma((2,)), dma((2,)), dma((G,)), dma((G,)), dma((G,)),
            dma((6, 2, NB)), dma((3, 2)), dma((2,)), dma((2,)), pltpu.SemaphoreType.REGULAR],
        compiler_params=pltpu.CompilerParams(collective_id=0, has_side_effects=True, vmem_limit_bytes=46 * 2**20),
    )(tiled, w_x.reshape(9, CH, 4 * CH), w_h.reshape(9, CH, 4 * CH), gate_bias.reshape(1, -1),
      h_init.reshape(S, R, HG, COLS, CH), c_init)
    h_all, c_final = pl.pallas_call(
        store,
        out_shape=(jax.ShapeDtypeStruct(tiled.shape, bf), jax.ShapeDtypeStruct(c_init.shape, f32)),
        in_specs=[vmem] * 4,
        out_specs=(hbm, hbm),
        scratch_shapes=[vm((2, R, HW, CH), f32), dma((4,))],
        compiler_params=pltpu.CompilerParams(vmem_limit_bytes=4 * 2**20),
    )(*[pltpu.with_memory_space_constraint(a, pltpu.VMEM) for a in parts])
    return h_all.reshape(frames.shape), c_final


def solution(mesh, K=None):
    n_rows = mesh.shape["rows"]
    frame_spec = P(None, "batch", "rows", "cols", None)
    state_spec = P("batch", "rows", "cols", None)
    blocks = BLOCKS if K is None else K
    return jax.shard_map(functools.partial(run, blocks, n_rows), mesh=mesh,
                         in_specs=(frame_spec, P(), P(), P(), state_spec, state_spec),
                         out_specs=(frame_spec, state_spec), check_vma=False)
```

profile of v0, /device:TPU:97, one launch (start us, length us, event | category | flops | bytes accessed | tf_op | source)
XLA Modules:
  0.0 45.9 jit_solution(5528792618430674494)
XLA Ops:
  0.6 41.4 %shard_map.77 = (bf16[16,32,8,8,64]{4,3,2,1,0:T(8,128)(2,1)S(1)}, bf16[16,32,4,8,64]{4,3,2,1,0:T(8,128)(2,1)S(1)}, f32[2,32,16,128]{3,2,1,0:T(8,128)S(1)}, f32[32,16,128]{2,1,0:T(8,128)S(1)}) custom-call(bf16[16,2,32,4,8,64]{5,4,3,2,1,0:T(8,128)(2,1)} %bitcast.6, bf16[9,64,256]{2,1,0:T(8,128)(2,1)} %bitcast.8, bf16[9,64,256]{2,1,0:T(8,128)(2,1)} %bitcast.9, ...), custom_call_target="tpu_custom_call" | custom-call | tf_op jit(solution)/shard_map/pallas_call | solution.py:460
  42.0 3.6 %shard_map.78 = (bf16[16,2,32,4,8,64]{5,4,3,2,1,0:T(8,128)(2,1)}, f32[2,32,32,64]{3,2,1,0:T(8,128)}) custom-call(bf16[16,32,8,8,64]{4,3,2,1,0:T(8,128)(2,1)S(1)} %get-tuple-element.8.hout, bf16[16,32,4,8,64]{4,3,2,1,0:T(8,128)(2,1)S(1)} %get-tuple-element.9.hpeer, f32[2,32,16,128]{3,2,1,0:T(8,128)S(1)} %get-tuple-element.10.cout, ...), custom_call_target="tpu_custom_call" | custom-call | tf_op jit(solution)/shard_map/pallas_call | solution.py:481
where the time goes:
time: 46.2 us; the launch traced here: 45.9 us
  Pallas kernels  45 us (97%)
  between operations  0.84 us (2%)
    pallas_call x1, Pallas kernels, run(): pl.pallas_call(functools.partial(kernel, plan, n_rows), out_shape=(vm((T,...  41.4 us
    pallas_call x1, Pallas kernels, run(): pl.pallas_call(store, out_shape=(jax.ShapeDtypeStruct(tiled.shape, bf), j...  3.64 us

commit v1 on v0

--- a/solution.py
+++ b/solution.py
@@ -40,7 +40,7 @@
         self.of = [(b, o) for b, k in enumerate(blocks) for o in range(k)]
         self.xrows = [blocks[b] - o for b, o in self.of]
         self.xat = [sum(self.xrows[:t]) for t in range(T + 1)]
-        self.parts = [[(0, 1), (1, 2), (2, 3), (3, k)] if b == 0 else [(0, k)] for b, k in enumerate(blocks)]
+        self.parts = [[(0, 1), (1, 2), (2, 4), (4, k)] if b == 0 else [(0, k)] for b, k in enumerate(blocks)]
         self.hat = [sum(blocks[:b]) for b in range(len(blocks) + 1)]
         self.cat = [sum(k - 1 for k in blocks[:b]) for b in range(len(blocks) + 1)]
         ends = [0, 1, 3, blocks[0] + 1, T]
@@ -336,9 +336,9 @@
                 both = [lax.select(keep, got, swapped), lax.select(keep, swapped, got)]
                 cbuf[PAD:PAD + R, theirs_c] = jnp.concatenate(both, axis=1)
                 pack_c(0)
-                pack_x(1, 3)
-                start_first(1, 0, 1, 3, 4)
-                start_first(0, 0, 1, 3, 4)
+                pack_x(1, 2)
+                start_first(1, 0, 1, 3)
+                start_first(0, 0, 1, 3)
                 first = 4
             if b == 0 and o == 2:
                 for at in pieces[:2]:
@@ -347,10 +347,10 @@
                 wait_x(2)
                 for at in pieces[2:4]:
                     piece(at, 9)
-                pack_x(3, k)
+                pack_x(2, k)
                 for side in range(2):
-                    start_first(side, 0, 5)
-                start_first(0, 1, 5)
+                    start_first(side, 0, 4, 5)
+                start_first(0, 1, 4, 5)
                 first = 4
             if b == 0 and o == 4:
                 for at in pieces[:2]:
@@ -367,7 +367,7 @@
             for at in pieces[first:]:
                 piece(at)
             if b == 0 and o == 0:
-                start_first(0, 1, 0, 2, 1, 3, 4)
+                start_first(0, 1, 0, 2, 1, 3)
             if o == 0 and b and not last:
                 pack_x(f + k, f + k + plan.blocks[b + 1])
         wait_border(b, 0, 2)
@@ -389,8 +389,8 @@
                 piece((f + o, lo, hi), 9 if o == 0 else 1)
                 if lo != top[0][0]:
                     continue
-                if b == 0 and o in (1, 2):
-                    wait_border(0, 3 + o)
+                if b == 0 and o in (1, 3):
+                    wait_border(0, 4 if o == 1 else 5)
                 if last and o == k // 2:
                     push_h(f, f + o)
                 if last and o == k - 2:

time: 46.2 us -> 46.2 us (level)
  no operation moved by 1% of the time
where the time goes in v1:
time: 46.2 us; the launch traced here: 45.9 us
  Pallas kernels  45 us (97%)
  between operations  0.84 us (2%)
    pallas_call x1, Pallas kernels, run(): pl.pallas_call(functools.partial(kernel, plan, n_rows), out_shape=(vm((T,...  41.4 us
    pallas_call x1, Pallas kernels, run(): pl.pallas_call(store, out_shape=(jax.ShapeDtypeStruct(tiled.shape, bf), j...  3.64 us

profile of v1, /device:TPU:97, one launch (start us, length us, event | category | flops | bytes accessed | tf_op | source)
XLA Modules:
  0.0 45.9 jit_solution(17704816237587780594)
XLA Ops:
  0.6 41.4 %shard_map.77 = (bf16[16,32,8,8,64]{4,3,2,1,0:T(8,128)(2,1)S(1)}, bf16[16,32,4,8,64]{4,3,2,1,0:T(8,128)(2,1)S(1)}, f32[2,32,16,128]{3,2,1,0:T(8,128)S(1)}, f32[32,16,128]{2,1,0:T(8,128)S(1)}) custom-call(bf16[16,2,32,4,8,64]{5,4,3,2,1,0:T(8,128)(2,1)} %bitcast.6, bf16[9,64,256]{2,1,0:T(8,128)(2,1)} %bitcast.8, bf16[9,64,256]{2,1,0:T(8,128)(2,1)} %bitcast.9, ...), custom_call_target="tpu_custom_call" | custom-call | tf_op jit(solution)/shard_map/pallas_call | solution.py:460
  42.0 3.6 %shard_map.78 = (bf16[16,2,32,4,8,64]{5,4,3,2,1,0:T(8,128)(2,1)}, f32[2,32,32,64]{3,2,1,0:T(8,128)}) custom-call(bf16[16,32,8,8,64]{4,3,2,1,0:T(8,128)(2,1)S(1)} %get-tuple-element.8.hout, bf16[16,32,4,8,64]{4,3,2,1,0:T(8,128)(2,1)S(1)} %get-tuple-element.9.hpeer, f32[2,32,16,128]{3,2,1,0:T(8,128)S(1)} %get-tuple-element.10.cout, ...), custom_call_target="tpu_custom_call" | custom-call | tf_op jit(solution)/shard_map/pallas_call | solution.py:481

commit v2 on v0

--- a/solution.py
+++ b/solution.py
@@ -14,7 +14,7 @@
 PIECE = 4
 RING = 8
 BLOCKS = (7, 9)
-LATE = (2, 3)
+LATE = (2, 4)
 BORDER = 3
 FAR = 16
 

time: 46.2 us -> 46.2 us (level)
  no operation moved by 1% of the time
where the time goes in v2:
time: 46.2 us; the launch traced here: 46 us
  Pallas kernels  45.2 us (98%)
  between operations  0.84 us (2%)
    pallas_call x1, Pallas kernels, run(): pl.pallas_call(functools.partial(kernel, plan, n_rows), out_shape=(vm((T,...  41.6 us
    pallas_call x1, Pallas kernels, run(): pl.pallas_call(store, out_shape=(jax.ShapeDtypeStruct(tiled.shape, bf), j...  3.64 us

profile of v2, /device:TPU:97, one launch (start us, length us, event | category | flops | bytes accessed | tf_op | source)
XLA Modules:
  0.0 46.0 jit_solution(12624609828267737791)
XLA Ops:
  0.6 41.6 %shard_map.77 = (bf16[16,32,8,8,64]{4,3,2,1,0:T(8,128)(2,1)S(1)}, bf16[16,32,4,8,64]{4,3,2,1,0:T(8,128)(2,1)S(1)}, f32[2,32,16,128]{3,2,1,0:T(8,128)S(1)}, f32[32,16,128]{2,1,0:T(8,128)S(1)}) custom-call(bf16[16,2,32,4,8,64]{5,4,3,2,1,0:T(8,128)(2,1)} %bitcast.6, bf16[9,64,256]{2,1,0:T(8,128)(2,1)} %bitcast.8, bf16[9,64,256]{2,1,0:T(8,128)(2,1)} %bitcast.9, ...), custom_call_target="tpu_custom_call" | custom-call | tf_op jit(solution)/shard_map/pallas_call | solution.py:460
  42.2 3.6 %shard_map.78 = (bf16[16,2,32,4,8,64]{5,4,3,2,1,0:T(8,128)(2,1)}, f32[2,32,32,64]{3,2,1,0:T(8,128)}) custom-call(bf16[16,32,8,8,64]{4,3,2,1,0:T(8,128)(2,1)S(1)} %get-tuple-element.8.hout, bf16[16,32,4,8,64]{4,3,2,1,0:T(8,128)(2,1)S(1)} %get-tuple-element.9.hpeer, f32[2,32,16,128]{3,2,1,0:T(8,128)S(1)} %get-tuple-element.10.cout, ...), custom_call_target="tpu_custom_call" | custom-call | tf_op jit(solution)/shard_map/pallas_call | solution.py:481
